TPU v7x, 32 devices: a whole 2x2x4 slice. The times are simulated.
32 devices in a mesh: dp: 8 (over z, x), tensor: 4 (over y, core).
Axes of the slice: x: 2, y: 2, z: 4, core: 2. Of those that a mesh axis runs over, the one named last changes fastest.
Arguments:
- block_input: float32 [8, 1280, 768], P('dp', 'tensor'), may hold values from -6 to 6
- passes: int32 [8], P('dp'), may hold values from 2 to 5, as said below
- pass_map: int32 [8, 1280], P('dp', 'tensor'), may hold values from 0 to 4, as said below
- pass_table: float32 [5, 768], replicated, may hold values from -5 to 5
- gain_one: float32 [768], replicated, may hold values from 0.1 to 1.9
- bias_one: float32 [768], replicated, may hold values from -3 to 3
- w_qkv: float32 [768, 3, 768], P(None, None, 'tensor'), may hold values from -0.21875 to 0.21875
- w_out: float32 [768, 768], P('tensor'), may hold values from -4 to 4
- gain_two: float32 [768], replicated, may hold values from 0.1 to 1.9
- bias_two: float32 [768], replicated, may hold values from -3 to 3
- w_up: float32 [768, 3072], P(None, 'tensor'), may hold values from -0.21875 to 0.21875
- w_down: float32 [3072, 768], P('tensor'), may hold values from -0.109375 to 0.109375
- grad_output: float32 [8, 1280, 768], P('dp', 'tensor'), may hold values from -6 to 6
Outputs:
- block_output: float32 [8, 1280, 768], P('dp', 'tensor')
- grad_input: float32 [8, 1280, 768], P('dp', 'tensor')
- grad_table: float32 [5, 768], P(None, 'dp')
- grad_gain_one: float32 [768], P('dp')
- grad_bias_one: float32 [768], P('dp')
- grad_qkv: float32 [768, 3, 768], P('dp', None, 'tensor')
- grad_out: float32 [768, 768], P('tensor', 'dp')
- grad_gain_two: float32 [768], P('dp')
- grad_bias_two: float32 [768], P('dp')
- grad_up: float32 [768, 3072], P('dp', 'tensor')
- grad_down: float32 [3072, 768], P('tensor', 'dp')
Inputs may be any that keep to these rules, and one draw needn't show every extreme that they name: Every draw has an item with 5 passes and an item with 2 passes. `pass_map`: slot s of an item with r passes holds s mod r.
All inputs are finite; a program needn't handle non-finite values.
Results may differ from a plain program's by a relative error of at most 0.0003.
Values sent between devices are 32-bit elements; how exact they have to be, the bound alone decides.
A program may use at most 128 MiB of HBM per device.

v0:
```python
import math
import functools
import jax
import jax.numpy as jnp
from jax import lax
from jax.experimental import pallas as pl
from jax.experimental.pallas import tpu as pltpu
from jax.sharding import PartitionSpec as P

f32 = jnp.float32
bf16 = jnp.bfloat16
HD = 64
BASE = 256
PASSES_MAX = 5
EPSILON = 1e-05
HUGE = 1e30
QB = 256
HIGH = lax.Precision.HIGH
MESH = pl.DeviceIdType.MESH
NN = (((1,), (0,)), ((), ()))
NT = (((1,), (1,)), ((), ()))
TN = (((0,), (0,)), ((), ()))


def mm(left, right, dims=NN):
    return lax.dot_general(left, right, dims, precision=HIGH, preferred_element_type=f32)


def bdot(left, right, dims=NN):
    return lax.dot_general(left, right, dims, preferred_element_type=f32)


def halves(value):
    high = value.astype(bf16)
    return high, (value - high.astype(f32)).astype(bf16)


def rcopy(src, dst, send, recv, where):
    return pltpu.make_async_remote_copy(
        src_ref=src, dst_ref=dst, send_sem=send, recv_sem=recv, device_id=where, device_id_type=MESH
    )


def places():
    t = lax.axis_index("tensor")
    sib = t + 1 - 2 * (t % 2)
    yp = (t + 2) % 4
    far = (sib + 2) % 4
    return t, sib, yp, far


def greet(others):
    barrier = pltpu.get_barrier_semaphore()
    for other in others:
        pl.semaphore_signal(barrier, inc=1, device_id=other, device_id_type=MESH)
    pl.semaphore_wait(barrier, len(others))


def order_of(n, owners):
    out = owners[0]
    for k in range(1, len(owners)):
        here = (n + len(owners) - k) // len(owners) - (n + len(owners) - k - 1) // len(owners)
        out = out + here * (owners[k] - owners[0])
    return out


def block(owner, rows, chunk=0, chunks=1):
    size = rows // chunks
    return pl.ds(pl.multiple_of(owner * rows + chunk * size, 8), size)


class Gather:
    def __init__(self, buf, send, recv, rows, chunks):
        t, sib, yp, far = places()
        self.own, self.yp, self.sib, self.far, self.rows, self.chunks = t, yp, sib, far, rows, chunks
        self.across, self.fwd = [], []
        mine = buf.at[block(t, rows)]
        self.side = rcopy(mine, mine, send.at[0], recv.at[0], {"tensor": sib})
        for k in range(chunks):
            part = buf.at[block(t, rows, k, chunks)]
            self.across.append(rcopy(part, part, send.at[1 + k], recv.at[1 + k], {"tensor": yp}))
            part = buf.at[block(yp, rows, k, chunks)]
            j = 1 + chunks + k
            self.fwd.append(rcopy(part, part, send.at[j], recv.at[j], {"tensor": sib}))

    def start(self):
        for c in self.across:
            c.start()
        self.side.start()

    def relay(self, k):
        self.across[k].wait_recv()
        self.fwd[k].start()

    def finish_sends(self):
        self.side.wait_send()
        for c in self.across + self.fwd:
            c.wait_send()


class Scatter:
    def __init__(self, part, own_in, pre_in, y_in, send, recv, rows, chunks):
        t, sib, yp, far = places()
        self.part, self.own_in, self.pre_in, self.y_in = part, own_in, pre_in, y_in
        self.rows, self.chunks, self.size = rows, chunks, rows // chunks
        self.t, self.sib, self.yp, self.far = t, sib, yp, far
        self.side = rcopy(part.at[block(sib, rows)], own_in, send.at[0], recv.at[0], {"tensor": sib})
        self.pre, self.across = [], []
        for k in range(chunks):
            here = pl.ds(k * self.size, self.size)
            self.pre.append(
                rcopy(part.at[block(far, rows, k, chunks)], pre_in.at[here], send.at[1 + k], recv.at[1 + k], {"tensor": sib})
            )
            j = 1 + chunks + k
            self.across.append(rcopy(pre_in.at[here], y_in.at[here], send.at[j], recv.at[j], {"tensor": yp}))

    def send_pre(self, k):
        self.pre[k].start()

    def send_across(self, k):
        self.pre[k].wait_recv()
        here = pl.ds(k * self.size, self.size)
        self.pre_in[here, :] = self.part[block(self.yp, self.rows, k, self.chunks), :] + self.pre_in[here, :]
        self.across[k].start()

    def send_side(self):
        self.side.start()

    def arrive(self):
        self.side.wait_recv()
        for c in self.across:
            c.wait_recv()

    def total(self, start, size):
        here = pl.ds(start, size)
        mine = pl.ds(pl.multiple_of(self.t * self.rows + start, 8), size)
        return self.part[mine, :] + self.own_in[here, :] + self.y_in[here, :]

    def finish_sends(self):
        self.side.wait_send()
        for c in self.pre + self.across:
            c.wait_send()


def slot_facts(start, passes_ref):
    count = passes_ref[0]
    slot = start + lax.broadcasted_iota(jnp.int32, (RS, 1), 0)
    which = jnp.zeros_like(slot)
    for r in range(1, PASSES_MAX + 1):
        which = jnp.where(count == r, slot % r, which)
    return which, jnp.where(slot < count * BASE, 1.0, 0.0)


def embed(x_ref, which, table_ref, here):
    rows = x_ref[here, :]
    added = jnp.zeros_like(rows)
    for p in range(PASSES_MAX):
        added = jnp.where(which == p, table_ref[pl.ds(p, 1), :], added)
    return rows + added


def norm_stats(values):
    center = values - jnp.mean(values, -1, keepdims=True)
    spread = jnp.mean(center * center, -1, keepdims=True)
    scale = lax.rsqrt(spread + EPSILON)
    return center * scale, scale


RS = 32


def over_rows(rows, body, size=RS):
    def step(i, carry):
        body(pl.multiple_of(i * size, size))
        return carry

    lax.fori_loop(0, rows // size, step, 0)


def cat_q(v):
    high = v.astype(bf16).astype(f32)
    low = v - high
    return jnp.concatenate([high, low, low, high], axis=1).astype(bf16)


def cat_k(v):
    high = v.astype(bf16).astype(f32)
    low = v - high
    return jnp.concatenate([high, low, high, low], axis=1).astype(bf16)


def fold(both):
    return both[:, :HD] + both[:, HD:]


def causal(s, size):
    row = lax.broadcasted_iota(jnp.int32, (QB, QB), 0)
    col = lax.broadcasted_iota(jnp.int32, (QB, QB), 1)
    last = jnp.where(col <= row, s[:, size - QB :], -HUGE)
    return last if size == QB else jnp.concatenate([s[:, : size - QB], last], axis=1)


def add_eight(ref, row, value):
    total = value[0:8, :]
    for k in range(1, value.shape[0] // 8):
        total = total + value[8 * k : 8 * k + 8, :]
    ref[pl.ds(row, 8), :] = ref[pl.ds(row, 8), :] + total


def row_of(ref):
    return ref[...].reshape(1, ref.shape[0])


def forward_kernel(
    dims, passes, x, table, g1, b1, g2, b2, go, w_h, wo_h,
    a_o, qc_o, kc_o, vc_o, o_o, lse_o, wq_o, h1_o, c_o, dz_o,
    A, DZ, QC, KC, VC, O, LSE, TOP, SUM, OT, PT, OWN, PRE, YIN, W3, WQ, WO,
    s1, r1, s2, r2, s3, r3, ls,
):
    rows, slots, feats, heads, chunks = dims
    t, sib, yp, far = places()
    mine0 = t * rows
    loads = [pltpu.make_async_copy(w_h, W3, ls.at[0]), pltpu.make_async_copy(wo_h, WO, ls.at[1])]
    for c in loads:
        c.start()
    gain, bias = row_of(g1), row_of(b1)

    def begin_rows(r):
        here = pl.ds(r, RS)
        which, live = slot_facts(mine0 + r, passes)
        h0 = embed(x, which, table, here)
        h1_o[here, :] = h0
        xhat, _ = norm_stats(h0)
        mine = pl.ds(pl.multiple_of(mine0 + r, RS), RS)
        A[mine, :] = xhat * gain + bias
        DZ[mine, :] = live * go[here, :]

    over_rows(rows, begin_rows)
    greet([{"tensor": sib}, {"tensor": yp}])
    ga = Gather(A, s1, r1, rows, chunks)
    gz = Gather(DZ, s2, r2, rows, chunks)
    ga.start()
    loads[0].wait()
    for c in range(3):
        WQ[c] = W3[:, c, :]
    outs = [pltpu.make_async_copy(WQ, wq_o, ls.at[2])]
    outs[0].start()

    def project(n, carry):
        @pl.when(n == 1)
        def _():
            ga.side.wait_recv()

        @pl.when(n == 2)
        def _():
            for k in range(chunks):
                ga.relay(k)
            gz.start()

        @pl.when(n == 3)
        def _():
            for k in range(chunks):
                ga.fwd[k].wait_recv()

        here = block(order_of(n, (t, sib, yp, far)), rows)
        for c, (ref, cat) in enumerate(((QC, cat_q), (KC, cat_k), (VC, cat_k))):
            pr = mm(A[here, :], WQ[c])
            if c == 0:
                pr = pr * (1.0 / math.sqrt(HD))
            for h in range(heads):
                ref[h, here, :] = cat(pr[:, h * HD : (h + 1) * HD])
        return carry

    lax.fori_loop(0, 4, project, 0)
    more = [
        pltpu.make_async_copy(A, a_o, ls.at[3]),
        pltpu.make_async_copy(QC, qc_o, ls.at[4]),
        pltpu.make_async_copy(KC, kc_o, ls.at[5]),
        pltpu.make_async_copy(VC, vc_o, ls.at[6]),
    ]
    for c in more:
        c.start()
    outs += more
    loads[1].wait()
    blocks = slots // QB
    row = lax.broadcasted_iota(jnp.int32, (QB, QB), 0)
    col = lax.broadcasted_iota(jnp.int32, (QB, QB), 1)
    upper = t // 2
    rs = Scatter(PT, OWN, PRE, YIN, s3, r3, rows, chunks)

    def attend(n, carry):
        i = upper * n + (1 - upper) * (blocks - 1 - n)
        q_rows = pl.ds(pl.multiple_of(i * QB, QB), QB)
        TOP[...] = jnp.full(TOP.shape, -HUGE, f32)
        SUM[...] = jnp.zeros(SUM.shape, f32)
        OT[...] = jnp.zeros(OT.shape, f32)

        def keys(j, inner):
            k_rows = pl.ds(pl.multiple_of(j * QB, QB), QB)
            ok = (row <= col) | (j < i)
            for h in range(heads):
                s = jnp.where(ok, bdot(KC[h, k_rows, :], QC[h, q_rows, :], NT), -HUGE)
                old = TOP[h]
                new = jnp.maximum(old, jnp.max(s, 0, keepdims=True))
                shrink = jnp.exp(old - new)
                p = jnp.exp(s - new)
                TOP[h] = new
                SUM[h] = SUM[h] * shrink + jnp.sum(p, 0, keepdims=True)
                ph, pw = halves(p)
                values = VC[h, k_rows, 0 : 2 * HD]
                OT[h] = OT[h] * shrink + (bdot(values, ph, TN) + bdot(values, pw, TN))
            return inner

        lax.fori_loop(0, i + 1, keys, 0)
        parts = []
        for h in range(heads):
            parts.append((OT[h, :HD, :] + OT[h, HD:, :]) / SUM[h])
            LSE[h, :, q_rows] = TOP[h] + jnp.log(SUM[h])
        o = jnp.concatenate(parts, axis=0).T
        O[q_rows, :] = o
        PT[q_rows, :] = mm(o, WO[...])

        @pl.when(n == 2)
        def _():
            for k in range(chunks):
                rs.send_pre(k)

        @pl.when(n == 3)
        def _():
            for k in range(chunks):
                rs.send_across(k)
            gz.side.wait_recv()

        return carry

    lax.fori_loop(0, blocks, attend, 0)
    rs.send_side()
    for k in range(chunks):
        gz.relay(k)
    more = [pltpu.make_async_copy(O, o_o, ls.at[7]), pltpu.make_async_copy(LSE, lse_o, ls.at[8])]
    for c in more:
        c.start()
    outs += more
    for k in range(chunks):
        gz.fwd[k].wait_recv()
    more = [pltpu.make_async_copy(DZ, dz_o, ls.at[9])]
    more[0].start()
    outs += more
    rs.arrive()
    gain2, bias2 = row_of(g2), row_of(b2)

    def end_rows(r):
        here = pl.ds(r, RS)
        _, live = slot_facts(mine0 + r, passes)
        h1 = h1_o[here, :] + live * rs.total(r, RS)
        h1_o[here, :] = h1
        xhat, _ = norm_stats(h1)
        c_o[here, :] = xhat * gain2 + bias2

    over_rows(rows, end_rows)
    for c in outs:
        c.wait()
    ga.finish_sends()
    gz.finish_sends()
    rs.finish_sends()


def struct(*shape):
    return jax.ShapeDtypeStruct(shape, f32)


def vm(*shape):
    return pltpu.VMEM(shape, f32)


def vb(*shape):
    return pltpu.VMEM(shape, bf16)


def pairs(count, *numbers):
    return [pltpu.SemaphoreType.DMA((n,)) for n in numbers for _ in range(count)]


IN_VMEM = pl.BlockSpec(memory_space=pltpu.VMEM)
IN_SMEM = pl.BlockSpec(memory_space=pltpu.SMEM)
IN_HBM = pl.BlockSpec(memory_space=pl.ANY)
CHUNKS = 2


def params(number):
    return pltpu.CompilerParams(collective_id=number, has_side_effects=True, vmem_limit_bytes=63 << 20)


def forward_call(passes, x, table, g1, b1, g2, b2, go, w, wo, slots):
    rows, feats = x.shape
    local = w.shape[2]
    heads = local // HD
    cat = jax.ShapeDtypeStruct((heads, slots, 4 * HD), bf16)
    ng = 1 + 2 * CHUNKS
    return pl.pallas_call(
        functools.partial(forward_kernel, (rows, slots, feats, heads, CHUNKS)),
        out_shape=(
            struct(slots, feats), cat, cat, cat, struct(slots, local), struct(heads, 1, slots), struct(3, feats, local),
            struct(rows, feats), struct(rows, feats), struct(slots, feats),
        ),
        in_specs=[IN_SMEM] + [IN_VMEM] * 7 + [IN_HBM] * 2,
        out_specs=(IN_HBM,) * 7 + (IN_VMEM, IN_VMEM, IN_HBM),
        scratch_shapes=[
            vm(slots, feats), vm(slots, feats),
            vb(heads, slots, 4 * HD), vb(heads, slots, 4 * HD), vb(heads, slots, 4 * HD),
            vm(slots, local), vm(heads, 1, slots), vm(heads, 1, QB), vm(heads, 1, QB), vm(heads, 2 * HD, QB), vm(slots, feats),
            vm(rows, feats), vm(rows, feats), vm(rows, feats),
            vm(feats, 3, local), vm(3, feats, local), vm(local, feats),
        ] + pairs(2, ng, ng, ng) + pairs(1, 10),
        compiler_params=params(1),
        name="forward_part",
    )(passes, x, table, g1, b1, g2, b2, go, w, wo)


def gelu_both(u):
    k = math.sqrt(2.0 / math.pi)
    square = u * u
    th = jnp.tanh(k * (u * (1.0 + 0.044715 * square)))
    half = 0.5 * (1.0 + th)
    slope = half + (0.5 * k) * u * (1.0 - th * th) * (1.0 + (3.0 * 0.044715) * square)
    return u * half, slope


def middle_kernel(
    dims, h1, go, g2, c_h, dz_h, wu_h, wd_h,
    dh1_o, vec_o, zp_o, gd_o, gu_o,
    C, DZ, ACT, DU, PT, OWN, PRE, YIN, WU, WD, GD, GU,
    s1, r1, s2, r2, ls,
):
    rows, slots, feats, chunks = dims
    t, sib, yp, far = places()
    first = pltpu.make_async_copy(c_h, C.at[block(t, rows)], ls.at[0])
    loads = [
        pltpu.make_async_copy(wd_h, WD, ls.at[1]),
        pltpu.make_async_copy(dz_h, DZ, ls.at[2]),
        pltpu.make_async_copy(wu_h, WU, ls.at[3]),
    ]
    first.start()
    for c in loads:
        c.start()
    greet([{"tensor": sib}, {"tensor": yp}])
    first.wait()
    gc = Gather(C, s1, r1, rows, chunks)
    gc.start()
    for c in loads:
        c.wait()

    def open_block(i, carry):
        here = block(i, rows)
        DU[here, :] = mm(DZ[here, :], WD[...], NT)
        return carry

    lax.fori_loop(0, slots // rows, open_block, 0)

    def work(here):
        act, slope = gelu_both(mm(C[here, :], WU[...]))
        ACT[here, :] = act
        du = DU[here, :] * slope
        DU[here, :] = du
        PT[here, :] = mm(du, WU[...], NT)

    rs = Scatter(PT, OWN, PRE, YIN, s2, r2, rows, chunks)

    def step(n, carry):
        @pl.when(n == 2)
        def _():
            gc.side.wait_recv()

        for k in range(chunks):

            @pl.when(n == 4 + 2 * k)
            def _():
                gc.relay(k)
                gc.fwd[k].wait_recv()

        late = n // 4
        k = late * ((n % 4) // 2) + (1 - late) * (n % 2)
        owner = late * ((n % 2) * yp + (1 - n % 2) * far) + (1 - late) * ((n // 2) * sib + (1 - n // 2) * t)
        here = pl.ds(pl.multiple_of(owner * rows + k * (rows // chunks), 8), rows // chunks)
        act, slope = gelu_both(mm(C[here, :], WU[...]))
        ACT[here, :] = act
        du = DU[here, :] * slope
        DU[here, :] = du
        PT[here, :] = mm(du, WU[...], NT)

        @pl.when(n == 3)
        def _():
            rs.send_side()

        for k in range(chunks):

            @pl.when(n == 4 + 2 * k)
            def _():
                rs.send_pre(k)

            @pl.when(n == 5 + 2 * k)
            def _():
                rs.send_across(k)

        return carry

    lax.fori_loop(0, 4 + 2 * chunks, step, 0)

    def grads(n, carry):
        cols = pl.ds(pl.multiple_of(n * 256, 256), 256)
        GU[cols, :] = mm(C[:, cols], DU[...], TN)
        GD[cols, :] = mm(DZ[:, cols], ACT[...], TN)
        return carry

    lax.fori_loop(0, feats // 256, grads, 0)
    gu_copy = pltpu.make_async_copy(GU, gu_o, ls.at[4])
    gu_copy.start()
    gd_copy = pltpu.make_async_copy(GD, gd_o, ls.at[5])
    gd_copy.start()

    def down(i, carry):
        here = block(i, rows)
        DZ[here, :] = mm(ACT[here, :], WD[...])
        return carry

    lax.fori_loop(0, slots // rows, down, 0)
    zp_copy = pltpu.make_async_copy(DZ, zp_o, ls.at[6])
    zp_copy.start()
    vec_o[...] = jnp.zeros_like(vec_o)
    gain2 = row_of(g2)
    rs.arrive()

    def end_rows(r):
        here = pl.ds(r, RS)
        dc = rs.total(r, RS)
        xhat, scale = norm_stats(h1[here, :])
        add_eight(vec_o, 0, dc * xhat)
        add_eight(vec_o, 8, dc)
        e = dc * gain2
        inner = e - jnp.mean(e, -1, keepdims=True) - xhat * jnp.mean(e * xhat, -1, keepdims=True)
        dh1_o[here, :] = go[here, :] + inner * scale

    over_rows(rows, end_rows)
    for c in (gu_copy, gd_copy, zp_copy):
        c.wait()
    gc.finish_sends()
    rs.finish_sends()


def middle_call(h1, go, g2, c, dz, wu, wd):
    rows, feats = h1.shape
    slots = dz.shape[0]
    hidden = wu.shape[1]
    ng = 1 + 2 * CHUNKS
    return pl.pallas_call(
        functools.partial(middle_kernel, (rows, slots, feats, CHUNKS)),
        out_shape=(struct(rows, feats), struct(16, feats), struct(slots, feats), struct(feats, hidden), struct(feats, hidden)),
        in_specs=[IN_VMEM] * 3 + [IN_HBM] * 4,
        out_specs=(IN_VMEM, IN_VMEM, IN_HBM, IN_HBM, IN_HBM),
        scratch_shapes=[
            vm(slots, feats), vm(slots, feats), vm(slots, hidden), vm(slots, hidden), vm(slots, feats),
            vm(rows, feats), vm(rows, feats), vm(rows, feats),
            vm(feats, hidden), vm(hidden, feats), vm(feats, hidden), vm(feats, hidden),
        ] + pairs(2, ng, ng) + pairs(1, 7),
        compiler_params=params(2),
        name="middle_part",
    )(h1, go, g2, c, dz, wu, wd)


FF_ORDERS = ((0, 1, 2), (1, 2, 0), (0, 1, 2), (0, 1, 2))
FF_START = (1, 0, 2, 3)
Q_ORDERS = ((0, 1, 2), (1, 0, 2), (0, 1, 2))


class Halve:
    def __init__(self, source, keep, in_one, in_two, in_three, send, recv, base, order):
        d = lax.axis_index("dp")
        bits = (d % 2, (d // 2) % 2, d // 4)
        peers = ({"dp": d + 1 - 2 * bits[0]}, {"dp": d + 2 - 4 * bits[1]}, {"dp": (d + 4) % 8})
        a1, a2, a3 = order
        self.mid, self.last = bits[a2], bits[a3]
        self.spot = (lambda x, y: 2 * x + y) if a2 > a3 else (lambda x, y: 2 * y + x)
        self.keep, self.ins = keep, (in_one, in_two, in_three)

        def whole(v, x, y):
            return v * 2**a1 + x * 2**a2 + y * 2**a3

        pick = [(x, y) for x in range(2) for y in range(2)]
        self.own = [(whole(bits[a1], x, y), self.spot(x, y)) for x, y in pick]
        self.one = [
            rcopy(source.at[whole(1 - bits[a1], x, y)], in_one.at[self.spot(x, y)], send.at[base + n], recv.at[base + n], peers[a1])
            for n, (x, y) in enumerate(pick)
        ]
        self.two = [
            rcopy(keep.at[self.spot(1 - self.mid, y)], in_two.at[y], send.at[base + 4 + y], recv.at[base + 4 + y], peers[a2])
            for y in range(2)
        ]
        self.three = rcopy(keep.at[self.spot(self.mid, 1 - self.last)], in_three, send.at[base + 6], recv.at[base + 6], peers[a3])

    def start_one(self):
        for c in self.one:
            c.start()

    def take_one(self):
        for c in self.one:
            c.wait_recv()
        self.keep[...] = self.keep[...] + self.ins[0][...]
        for c in self.two:
            c.start()

    def take_two(self):
        for y in range(2):
            self.two[y].wait_recv()
            at = self.spot(self.mid, y)
            self.keep[at] = self.keep[at] + self.ins[1][y]
        self.three.start()

    def take_three(self):
        self.three.wait_recv()
        return self.keep[self.spot(self.mid, self.last)] + self.ins[2][...]

    def finish_sends(self):
        for c in self.one + self.two + [self.three]:
            c.wait_send()


def backward_kernel(dims, *refs):
    rows, slots, feats, heads, chunks, halving = dims
    refs = list(refs)

    def take(n):
        out = refs[:n]
        del refs[:n]
        return out

    passes, x, table, g1, h1, dh1, vec2 = take(7)
    qc_h, kc_h, vc_h, o_h, lse_h, a_h, zp_h, wq_h, wo_h = take(9)
    if halving:
        gd_h, gu_h = take(2)
    out_o, gi_o, vec_o, gt_o, gq_o = take(5)
    if halving:
        gd_o, gu_o = take(2)
    QC, KC, VC, DOC, LSE, DROW, DATT, DQ, DK, DV, DP = take(11)
    OWN, PRE, YIN, ZP, ZOWN, ZPRE, ZYIN, WQ, WO, ACC, VB, VIN = take(12)
    if halving:
        GT, GQ, KF, KT, KQ, F1, F2, F3, T1, T2, T3, Q1, Q2, Q3 = take(14)
    s1, r1, s2, r2, s3, r3, sv, rv, ls = take(9)
    if halving:
        sh, rh = take(2)
    O = DP.at[0]
    t, sib, yp, far = places()
    mine0 = t * rows
    loads = [
        pltpu.make_async_copy(src, dst, ls.at[n])
        for n, (src, dst) in enumerate(
            ((wo_h, WO), (o_h, DP.at[0]), (zp_h, ZP), (qc_h, QC), (kc_h, KC), (vc_h, VC), (lse_h, LSE), (wq_h, WQ))
        )
    ]
    if halving:
        d = lax.axis_index("dp")
        low = d % 2
        width = KF.shape[-1]
        pieces = [(ref, k) for ref in (gu_h, gd_h) for k in range(ref.shape[-1] // width)]
        hf = []
        for n, (ref, k) in enumerate(pieces):
            ref = ref.at[:, :, pl.ds(k * width, width)]
            hf.append(Halve(ref, KF.at[n], F1.at[n], F2.at[n], F3.at[n], sh, rh, 7 * n, FF_ORDERS[n]))
            loads += [
                pltpu.make_async_copy(ref.at[a], KF.at[n, b], ls.at[9 + 4 * n + m]) for m, (a, b) in enumerate(hf[n].own)
            ]
        early = loads[8:]
    for c in loads:
        c.start()

    def begin_rows(r):
        here = pl.ds(r, RS)
        _, live = slot_facts(mine0 + r, passes)
        DATT[pl.ds(pl.multiple_of(mine0 + r, RS), RS), :] = live * dh1[here, :]

    over_rows(rows, begin_rows)
    others = [{"tensor": sib}, {"tensor": yp}]
    if halving:
        others += [{"dp": d + 1 - 2 * low}, {"dp": d + 2 - 4 * ((d // 2) % 2)}, {"dp": (d + 4) % 8}]
    greet(others)
    gt = Gather(DATT, s1, r1, rows, chunks)
    gt.start()
    if halving:
        for n in FF_START:
            hf[n].start_one()
        base = 7 * len(pieces)
        ht = Halve(GT, KT, T1, T2, T3, sh, rh, base, (0, 1, 2))
        hq = [Halve(GQ.at[c], KQ.at[c], Q1.at[c], Q2.at[c], Q3.at[c], sh, rh, base + 7 + 7 * c, Q_ORDERS[c]) for c in range(3)]

        def ff_out(n):
            k = n % (len(pieces) // 2)
            if n < len(pieces) // 2:
                gu_o[:, k * width : (k + 1) * width] = hf[n].take_three()
            else:
                gd_o[k * width : (k + 1) * width, :] = hf[n].take_three().T
    rz = Scatter(ZP, ZOWN, ZPRE, ZYIN, s2, r2, rows, chunks)
    loads[2].wait()
    for k in range(chunks):
        rz.send_pre(k)
    rz.send_side()
    loads[0].wait()

    def mixed_grad(n, carry):
        @pl.when(n == 1)
        def _():
            gt.side.wait_recv()

        @pl.when(n == 2)
        def _():
            for k in range(chunks):
                gt.relay(k)
            for k in range(chunks):
                rz.send_across(k)
            if halving:
                for c in early:
                    c.wait()
                hf[0].take_one()
                hf[1].take_one()

        @pl.when(n == 3)
        def _():
            for k in range(chunks):
                gt.fwd[k].wait_recv()

        here = block(order_of(n, (t, sib, yp, far)), rows)
        do = mm(DATT[here, :], WO[...], NT)
        for h in range(heads):
            DOC[h, here, :] = cat_q(do[:, h * HD : (h + 1) * HD])
        return carry

    lax.fori_loop(0, 4, mixed_grad, 0)
    loads[1].wait()
    grad_out = mm(DATT[...], O[...], TN)
    for c in loads[3:8]:
        c.wait()
    if halving:
        GT[...] = grad_out.reshape(GT.shape)
        for a, b in ht.own:
            KT[b] = GT[a]
        ht.start_one()
    else:
        gt_o[...] = grad_out
    gt.finish_sends()
    blocks = slots // QB
    row = lax.broadcasted_iota(jnp.int32, (QB, QB), 0)
    col = lax.broadcasted_iota(jnp.int32, (QB, QB), 1)
    ones = jnp.ones((8, HD), f32)
    for i in reversed(range(blocks)):
        q_rows = pl.ds(i * QB, QB)
        size = (i + 1) * QB
        k_rows = pl.ds(0, size)
        for h in range(heads):
            do = fold(DOC[h, q_rows, 0 : 2 * HD].astype(f32))
            DROW[h] = mm(ones, do * O[q_rows, h * HD : (h + 1) * HD], NT)

        def one_head(h, carry):
            q, do = QC[h, q_rows, :], DOC[h, q_rows, :]
            s = bdot(KC[h, k_rows, :], q, NT)
            last = jnp.where(row <= col, s[size - QB :, :], -HUGE)
            s = last if i == 0 else jnp.concatenate([s[: size - QB, :], last], axis=0)
            p = jnp.exp(s - LSE[h, :, q_rows])
            ds = p * (bdot(VC[h, k_rows, :], do, NT) - DROW[h, 0:1, :])
            ph, pw = halves(p)
            dsh, dsw = halves(ds)
            do2, q2 = do[:, : 2 * HD], q[:, : 2 * HD]
            dv = bdot(ph, do2) + bdot(pw, do2)
            dk = bdot(dsh, q2) + bdot(dsw, q2)
            keys = KC[h, k_rows, 0 : 2 * HD]
            DQ[h, :, :] = bdot(dsh, keys, TN) + bdot(dsw, keys, TN)
            if i == blocks - 1:
                DV[h, :, :] = dv
                DK[h, :, :] = dk
            else:
                DV[h, k_rows, :] = DV[h, k_rows, :] + dv
                DK[h, k_rows, :] = DK[h, k_rows, :] + dk
            return carry

        lax.fori_loop(0, heads, one_head, 0)
        dq = jnp.concatenate([fold(DQ[h]) for h in range(heads)], axis=1)
        DP[0, q_rows, :] = dq * (1.0 / math.sqrt(HD))
        if halving and i == 4:
            hf[0].take_two()
            hf[1].take_two()
        if halving and i == 3:
            hf[2].take_one()
        if halving and i == 2:
            ff_out(0)
        if halving and i == 1:
            ff_out(1)
            hf[2].take_two()
        if halving and i == 0:
            hf[3].take_one()
    rd = Scatter(DATT, OWN, PRE, YIN, s3, r3, rows, chunks)

    def head_grads(n, carry):
        here = block(order_of(n, (far, yp, sib, t)), rows)
        total = mm(DP[0, here, :], WQ[0], NT)
        for c, ref in ((1, DK), (2, DV)):
            part = jnp.concatenate([fold(ref[h, here, :]) for h in range(heads)], axis=1)
            DP[c, here, :] = part
            total = total + mm(part, WQ[c], NT)
        DATT[here, :] = total

        @pl.when(n == 0)
        def _():
            for k in range(chunks):
                rd.send_pre(k)

        @pl.when(n == 1)
        def _():
            for k in range(chunks):
                rd.send_across(k)

        @pl.when(n == 2)
        def _():
            rd.send_side()

        return carry

    lax.fori_loop(0, 4, head_grads, 0)
    rz.arrive()

    def out_rows(r):
        here = pl.ds(r, RS)
        _, live = slot_facts(mine0 + r, passes)
        out_o[here, :] = h1[here, :] + live * rz.total(r, RS)

    over_rows(rows, out_rows)
    rz.finish_sends()
    a_copy = pltpu.make_async_copy(a_h, ZP, ls.at[8])
    a_copy.start()
    a_copy.wait()

    def weight_grads(c, carry):
        full = mm(ZP[...], DP[c], TN)
        if not halving:
            gq_o[c] = full
            return carry
        GQ[c] = full.reshape(GQ.shape[1:])
        for k in range(3):

            @pl.when(c == k)
            def _():
                for a, b in hq[k].own:
                    KQ[k, b] = GQ[k, a]
                hq[k].start_one()

        return carry

    lax.fori_loop(0, 3, weight_grads, 0)
    if halving:
        hf[3].take_two()
        ff_out(2)
        ht.take_one()
        hq[1].take_one()
        hq[0].take_one()
        ff_out(3)
        ht.take_two()
        hq[1].take_two()
        hq[0].take_two()
        hq[2].take_one()
        gt_o[...] = ht.take_three().T
    ACC[...] = jnp.zeros_like(ACC)
    gain1 = row_of(g1)
    rd.arrive()

    def end_rows(r):
        here = pl.ds(r, RS)
        which, _ = slot_facts(mine0 + r, passes)
        xhat, scale = norm_stats(embed(x, which, table, here))
        da = rd.total(r, RS)
        add_eight(ACC, 0, da * xhat)
        add_eight(ACC, 8, da)
        e = da * gain1
        inner = e - jnp.mean(e, -1, keepdims=True) - xhat * jnp.mean(e * xhat, -1, keepdims=True)
        gi = dh1[here, :] + inner * scale
        gi_o[here, :] = gi
        for p in range(PASSES_MAX):
            add_eight(ACC, 16 + 8 * p, jnp.where(which == p, gi, 0.0))

    over_rows(rows, end_rows)
    VB[0] = jnp.zeros_like(VB[0])
    for n in range(2):
        VB[0, pl.ds(n, 1), :] = jnp.sum(ACC[8 * n : 8 * n + 8, :], 0, keepdims=True)
        VB[0, pl.ds(2 + n, 1), :] = jnp.sum(vec2[8 * n : 8 * n + 8, :], 0, keepdims=True)
    for p in range(PASSES_MAX):
        VB[0, pl.ds(4 + p, 1), :] = jnp.sum(ACC[16 + 8 * p : 24 + 8 * p, :], 0, keepdims=True)
    rounds = []
    for n, other in enumerate(others):
        c = rcopy(VB.at[n], VIN.at[n], sv.at[n], rv.at[n], other)
        c.start()
        if halving and n == 0:
            hq[2].take_two()
        if halving and n == 1:
            gq_o[:, 0, :] = hq[0].take_three()
        if halving and n == 2:
            gq_o[:, 1, :] = hq[1].take_three()
        c.wait_recv()
        VB[n + 1] = VB[n] + VIN[n]
        rounds.append(c)
    if halving:
        share = feats // 8
        for k in range(8):

            @pl.when(d == k)
            def _():
                vec_o[...] = VB[len(others), :, k * share : (k + 1) * share]

        gq_o[:, 2, :] = hq[2].take_three()
        for h in hf + [ht] + hq:
            h.finish_sends()
    else:
        vec_o[...] = VB[len(others)]
    for c in rounds:
        c.wait_send()
    rd.finish_sends()


def backward_call(passes, x, table, g1, h1, dh1, vec2, qc, kc, vc, o, lse, a, zp, wq, wo, gd, gu, halving):
    rows, feats = x.shape
    slots, local = o.shape
    heads = local // HD
    hidden = gd.shape[1]
    ng = 1 + 2 * CHUNKS
    ends = 5 if halving else 2
    share = feats // 8
    cat = vb(heads, slots, 4 * HD)
    wide = vm(heads, slots, 2 * HD)
    outs = [struct(rows, feats), struct(rows, feats), struct(16, share if halving else feats)]
    args = [passes, x, table, g1, h1, dh1, vec2, qc, kc, vc, o, lse, a, zp, wq, wo]
    scratch = [
        cat, cat, cat, cat, vm(heads, 1, slots), vm(heads, 8, QB), vm(slots, feats), vm(heads, QB, 2 * HD), wide, wide, vm(3, slots, local),
        vm(rows, feats), vm(rows, feats), vm(rows, feats), vm(slots, feats), vm(rows, feats), vm(rows, feats), vm(rows, feats),
        vm(3, feats, local), vm(local, feats), vm(16 + 8 * PASSES_MAX, feats), vm(ends + 1, 16, feats), vm(ends, 16, feats),
    ]
    sems = pairs(2, ng, ng, ng, ends) + pairs(1, 25)
    if halving:
        outs += [struct(local, share), struct(share, 3, local), struct(hidden, share), struct(share, hidden)]
        args += [gd.reshape(8, share, hidden), gu.reshape(8, share, hidden)]
        scratch += [vm(8, share, local), vm(3, 8, share, local)]
        width = hidden // 2
        scratch += [vm(4, 4, share, width), vm(4, share, local), vm(3, 4, share, local)]
        scratch += [vm(4, 4, share, width), vm(4, 2, share, width), vm(4, share, width)]
        scratch += [vm(4, share, local), vm(2, share, local), vm(share, local)]
        scratch += [vm(3, 4, share, local), vm(3, 2, share, local), vm(3, share, local)]
        sems += pairs(2, 56)
    else:
        outs += [struct(feats, local), struct(3, feats, local)]
    return pl.pallas_call(
        functools.partial(backward_kernel, (rows, slots, feats, heads, CHUNKS, halving)),
        out_shape=tuple(outs),
        in_specs=[IN_SMEM] + [IN_VMEM] * 6 + [IN_HBM] * (len(args) - 7),
        out_specs=(IN_VMEM,) * len(outs),
        scratch_shapes=scratch + sems,
        compiler_params=params(3),
        name="backward_part",
    )(*args)


def per_device(
    block_input, passes, pass_map, pass_table, gain_one, bias_one, w_qkv, w_out, gain_two, bias_two, w_up, w_down, grad_output
):
    x, go = block_input[0], grad_output[0]
    rows, feats = x.shape
    slots = rows * lax.axis_size("tensor")
    ways = lax.axis_size("dp")
    halving = ways == 8
    a, qc, kc, vc, o, lse, wq, h1, c, dz = forward_call(
        passes, x, pass_table, gain_one, bias_one, gain_two, bias_two, go, w_qkv, w_out, slots
    )
    dh1, vec2, zp, gd, gu = middle_call(h1, go, gain_two, c, dz, w_up, w_down)
    got = backward_call(passes, x, pass_table, gain_one, h1, dh1, vec2, qc, kc, vc, o, lse, a, zp, wq, w_out, gd, gu, halving)
    out, gi, part, gt, gq = got[:5]
    if halving:
        gd, gu = got[5:]
    else:
        gq = jnp.swapaxes(gq, 0, 1)
        gt, gq, gu, gd = (lax.psum_scatter(v, "dp", scatter_dimension=0, tiled=True) for v in (gt, gq, gu, gd))
        part = lax.psum_scatter(part, "dp", scatter_dimension=1, tiled=True)
        gt, gd = gt.T, gd.T
    return (
        out[None], gi[None], part[4 : 4 + PASSES_MAX], part[0], part[1], gq, gt, part[2], part[3], gu, gd,
    )


def solution(mesh):
    placed = (
        P("dp", "tensor", None), P("dp"), P("dp", "tensor"), P(), P(), P(), P(None, None, "tensor"), P("tensor", None),
        P(), P(), P(None, "tensor"), P("tensor", None), P("dp", "tensor", None),
    )
    return jax.shard_map(
        per_device,
        mesh=mesh,
        in_specs=placed,
        out_specs=(
            P("dp", "tensor", None), P("dp", "tensor", None), P(None, "dp"), P("dp"), P("dp"), P("dp", None, "tensor"),
            P("tensor", "dp"), P("dp"), P("dp"), P("dp", "tensor"), P("tensor", "dp"),
        ),
        check_vma=False,
    )
```

profile of v0, /device:TPU:0, one launch (start us, length us, event | category | flops | bytes accessed | tf_op | source)
XLA Modules:
  0.0 266.5 jit_solution(7612808088641421030)
XLA Ops:
  1.3 4.2 %copy.23.w_h = f32[768,3,192]{2,1,0:T(4,128)} copy(f32[768,3,192]{0,2,1:T(8,128)} %param.18) | data formatting | bytes 3538944 | tf_op args[6]
  5.5 76.1 %forward_part.1 = (f32[1280,768]{1,0:T(8,128)}, bf16[3,1280,256]{2,1,0:T(8,128)(2,1)}, bf16[3,1280,256]{2,1,0:T(8,128)(2,1)}, bf16[3,1280,256]{2,1,0:T(8,128)(2,...) custom-call(s32[1]{0:T(128)S(6)} %copy.30.passes.refs_0_, ...), custom_call_target="tpu_custom_call" | custom-call | tf_op jit(solution)/shard_map/forward_part/pallas_call | solution.py:400
  81.7 55.0 %middle_part.1 = (f32[320,768]{1,0:T(8,128)}, f32[16,768]{1,0:T(8,128)}, f32[1280,768]{1,0:T(8,128)}, f32[768,768]{1,0:T(8,128)}, f32[768,768]{1,0:T(8,128)}) custom-call(f32[320,768]{1,0:T(8,128)} %get-tuple-element.33.h1.refs_4_, f32[320,768]{1,0:T(8,128)} %bitcast.17, f32[768]{0:T(1024)} %g2.3, f32[320,768]{1,0:T(8,128)} %get-tuple-element.34.c_h, ...), custom_call_target="tpu_custom_call" | custom-call | tf_op jit(solution)/shard_map/middle_part/pallas_call | solution.py:555
  136.7 119.0 %backward_part.1 = (f32[320,768]{1,0:T(8,128)}, f32[320,768]{1,0:T(8,128)}, f32[16,96]{1,0:T(8,128)}, f32[192,96]{1,0:T(8,128)}, f32[96,3,192]{2,1,0:T(4,128)}, /*index=5*/f32[768,96]{1,0:T(8,128)}, f32[96,768]{1,0:T(8,128)}) custom-call(s32[1]{0:T(128)S(6)} %copy.30.passes.refs_0_, f32[320,768]{1,0:T(8,128)} %bitcast.15, f32[5,768]{1,0:T(8,128)} %refs_2_.1, ...), custom_call_target="tpu_custom_call" | custom-call | tf_op jit(solution)/shard_map/backward_part/pallas_call | solution.py:953
  255.7 0.0 copy-start
  255.7 1.4 slice_bitcast_fusion
  257.0 1.3 slice.15
  258.3 1.8 copy.24
  260.1 0.0 copy-start.2
  260.1 0.0 copy-start.1
  260.1 1.9 copy.25
  262.0 2.2 copy.31
  264.2 0.0 copy-done
  264.2 0.9 copy.32
  265.2 0.0 copy-done.2
  265.2 0.6 copy.33
  265.8 0.0 copy-done.1
  265.8 0.7 copy.34
Async XLA Ops:
  255.7 8.6 %copy-start = (f32[320,768]{1,0:T(8,128)S(1)}, f32[320,768]{1,0:T(8,128)}, u32[]{:S(2)}) copy-start(f32[320,768]{1,0:T(8,128)} %get-tuple-element.49) | copy-start | bytes 2949124
  260.1 5.1 %copy-start.2 = (f32[192,96]{1,0:T(8,128)S(1)}, f32[192,96]{1,0:T(8,128)}, u32[]{:S(2)}) copy-start(f32[192,96]{1,0:T(8,128)} %get-tuple-element.87) | copy-start | bytes 221188
  260.1 5.7 %copy-start.1 = (f32[96,768]{1,0:T(8,128)S(1)}, f32[96,768]{1,0:T(8,128)}, u32[]{:S(2)}) copy-start(f32[96,768]{1,0:T(8,128)} %get-tuple-element.90) | copy-start | bytes 884740
where the time goes:
time: 267 us
  Pallas kernels  250 us (94%)
  local copies, waits for them, and re-layouts  15.1 us (6%)
    pallas_call x1, Pallas kernels, backward_call(): pl.pallas_call(functools.partial(backward_kernel, (rows, slots, feats, he...  119 us
    pallas_call x1, Pallas kernels, forward_call(): pl.pallas_call(functools.partial(forward_kernel, (rows, slots, feats, hea...  76.1 us
    pallas_call x1, Pallas kernels, middle_call(): pl.pallas_call(functools.partial(middle_kernel, (rows, slots, feats, CHUN...  55 us
    unnamed x13, local copies, waits for them, and re-layouts  12.4 us

commit v1 on v0

--- a/solution.py
+++ b/solution.py
@@ -50,10 +50,12 @@
 
 
 def greet(others):
-    barrier = pltpu.get_barrier_semaphore()
     for other in others:
-        pl.semaphore_signal(barrier, inc=1, device_id=other, device_id_type=MESH)
-    pl.semaphore_wait(barrier, len(others))
+        pl.semaphore_signal(pltpu.get_barrier_semaphore(), inc=1, device_id=other, device_id_type=MESH)
+
+
+def met(others):
+    pl.semaphore_wait(pltpu.get_barrier_semaphore(), len(others))
 
 
 def order_of(n, owners):
@@ -70,15 +72,16 @@
 
 
 class Gather:
-    def __init__(self, buf, send, recv, rows, chunks):
+    def __init__(self, buf, send, recv, rows, chunks, source=None):
         t, sib, yp, far = places()
         self.own, self.yp, self.sib, self.far, self.rows, self.chunks = t, yp, sib, far, rows, chunks
         self.across, self.fwd = [], []
         mine = buf.at[block(t, rows)]
-        self.side = rcopy(mine, mine, send.at[0], recv.at[0], {"tensor": sib})
+        self.side = rcopy(mine if source is None else source, mine, send.at[0], recv.at[0], {"tensor": sib})
         for k in range(chunks):
             part = buf.at[block(t, rows, k, chunks)]
-            self.across.append(rcopy(part, part, send.at[1 + k], recv.at[1 + k], {"tensor": yp}))
+            first = part if source is None else source.at[pl.ds(k * (rows // chunks), rows // chunks)]
+            self.across.append(rcopy(first, part, send.at[1 + k], recv.at[1 + k], {"tensor": yp}))
             part = buf.at[block(yp, rows, k, chunks)]
             j = 1 + chunks + k
             self.fwd.append(rcopy(part, part, send.at[j], recv.at[j], {"tensor": sib}))
@@ -212,39 +215,47 @@
 
 
 def forward_kernel(
-    dims, passes, x, table, g1, b1, g2, b2, go, w_h, wo_h,
-    a_o, qc_o, kc_o, vc_o, o_o, lse_o, wq_o, h1_o, c_o, dz_o,
-    A, DZ, QC, KC, VC, O, LSE, TOP, SUM, OT, PT, OWN, PRE, YIN, W3, WQ, WO,
+    dims, passes, x, table, g1, b1, g2, b2, go, wq_h, wo_h,
+    a_o, qc_o, kc_o, vc_o, o_o, lse_o, h1_o, c_o, dz_o,
+    A, DZ, QC, KC, VC, O, LSE, TOP, SUM, OT, PT, OWN, PRE, YIN, WQ, WO,
     s1, r1, s2, r2, s3, r3, ls,
 ):
     rows, slots, feats, heads, chunks = dims
     t, sib, yp, far = places()
     mine0 = t * rows
-    loads = [pltpu.make_async_copy(w_h, W3, ls.at[0]), pltpu.make_async_copy(wo_h, WO, ls.at[1])]
+    loads = [pltpu.make_async_copy(wq_h, WQ, ls.at[0]), pltpu.make_async_copy(wo_h, WO, ls.at[1])]
     for c in loads:
         c.start()
     gain, bias = row_of(g1), row_of(b1)
 
+    others = [{"tensor": sib}, {"tensor": yp}]
+    greet(others)
+    ga = Gather(A, s1, r1, rows, chunks)
+    gz = Gather(DZ, s2, r2, rows, chunks)
+
     def begin_rows(r):
         here = pl.ds(r, RS)
-        which, live = slot_facts(mine0 + r, passes)
+        which, _ = slot_facts(mine0 + r, passes)
         h0 = embed(x, which, table, here)
         h1_o[here, :] = h0
         xhat, _ = norm_stats(h0)
-        mine = pl.ds(pl.multiple_of(mine0 + r, RS), RS)
-        A[mine, :] = xhat * gain + bias
-        DZ[mine, :] = live * go[here, :]
-
-    over_rows(rows, begin_rows)
-    greet([{"tensor": sib}, {"tensor": yp}])
-    ga = Gather(A, s1, r1, rows, chunks)
-    gz = Gather(DZ, s2, r2, rows, chunks)
-    ga.start()
+        A[pl.ds(pl.multiple_of(mine0 + r, RS), RS), :] = xhat * gain + bias
+
+    over_rows(rows // 2, begin_rows)
+    met(others)
+    ga.across[0].start()
+    over_rows(rows // 2, lambda r: begin_rows(r + rows // 2))
+    ga.across[1].start()
+    ga.side.start()
+
+    def mask_rows(r):
+        here = pl.ds(r, RS)
+        _, live = slot_facts(mine0 + r, passes)
+        DZ[pl.ds(pl.multiple_of(mine0 + r, RS), RS), :] = live * go[here, :]
+
+    over_rows(rows, mask_rows)
     loads[0].wait()
-    for c in range(3):
-        WQ[c] = W3[:, c, :]
-    outs = [pltpu.make_async_copy(WQ, wq_o, ls.at[2])]
-    outs[0].start()
+    outs = []
 
     def project(n, carry):
         @pl.when(n == 1)
@@ -264,7 +275,7 @@
 
         here = block(order_of(n, (t, sib, yp, far)), rows)
         for c, (ref, cat) in enumerate(((QC, cat_q), (KC, cat_k), (VC, cat_k))):
-            pr = mm(A[here, :], WQ[c])
+            pr = mm(A[here, :], WQ[c], NT)
             if c == 0:
                 pr = pr * (1.0 / math.sqrt(HD))
             for h in range(heads):
@@ -391,30 +402,30 @@
     return pltpu.CompilerParams(collective_id=number, has_side_effects=True, vmem_limit_bytes=63 << 20)
 
 
-def forward_call(passes, x, table, g1, b1, g2, b2, go, w, wo, slots):
+def forward_call(passes, x, table, g1, b1, g2, b2, go, wq, wo, slots):
     rows, feats = x.shape
-    local = w.shape[2]
+    local = wq.shape[1]
     heads = local // HD
     cat = jax.ShapeDtypeStruct((heads, slots, 4 * HD), bf16)
     ng = 1 + 2 * CHUNKS
     return pl.pallas_call(
         functools.partial(forward_kernel, (rows, slots, feats, heads, CHUNKS)),
         out_shape=(
-            struct(slots, feats), cat, cat, cat, struct(slots, local), struct(heads, 1, slots), struct(3, feats, local),
+            struct(slots, feats), cat, cat, cat, struct(slots, local), struct(heads, 1, slots),
             struct(rows, feats), struct(rows, feats), struct(slots, feats),
         ),
         in_specs=[IN_SMEM] + [IN_VMEM] * 7 + [IN_HBM] * 2,
-        out_specs=(IN_HBM,) * 7 + (IN_VMEM, IN_VMEM, IN_HBM),
+        out_specs=(IN_HBM,) * 6 + (IN_VMEM, IN_VMEM, IN_HBM),
         scratch_shapes=[
             vm(slots, feats), vm(slots, feats),
             vb(heads, slots, 4 * HD), vb(heads, slots, 4 * HD), vb(heads, slots, 4 * HD),
             vm(slots, local), vm(heads, 1, slots), vm(heads, 1, QB), vm(heads, 1, QB), vm(heads, 2 * HD, QB), vm(slots, feats),
             vm(rows, feats), vm(rows, feats), vm(rows, feats),
-            vm(feats, 3, local), vm(3, feats, local), vm(local, feats),
+            vm(3, local, feats), vm(local, feats),
         ] + pairs(2, ng, ng, ng) + pairs(1, 10),
         compiler_params=params(1),
         name="forward_part",
-    )(passes, x, table, g1, b1, g2, b2, go, w, wo)
+    )(passes, x, table, g1, b1, g2, b2, go, wq, wo)
 
 
 def gelu_both(u):
@@ -443,10 +454,12 @@
     first.start()
     for c in loads:
         c.start()
-    greet([{"tensor": sib}, {"tensor": yp}])
+    others = [{"tensor": sib}, {"tensor": yp}]
+    greet(others)
+    gc = Gather(C, s1, r1, rows, chunks, c_h)
+    met(others)
+    gc.start()
     first.wait()
-    gc = Gather(C, s1, r1, rows, chunks)
-    gc.start()
     for c in loads:
         c.wait()
 
@@ -672,16 +685,18 @@
     for c in loads:
         c.start()
 
+    others = [{"tensor": sib}, {"tensor": yp}]
+    if halving:
+        others += [{"dp": d + 1 - 2 * low}, {"dp": d + 2 - 4 * ((d // 2) % 2)}, {"dp": (d + 4) % 8}]
+    greet(others)
+
     def begin_rows(r):
         here = pl.ds(r, RS)
         _, live = slot_facts(mine0 + r, passes)
         DATT[pl.ds(pl.multiple_of(mine0 + r, RS), RS), :] = live * dh1[here, :]
 
     over_rows(rows, begin_rows)
-    others = [{"tensor": sib}, {"tensor": yp}]
-    if halving:
-        others += [{"dp": d + 1 - 2 * low}, {"dp": d + 2 - 4 * ((d // 2) % 2)}, {"dp": (d + 4) % 8}]
-    greet(others)
+    met(others)
     gt = Gather(DATT, s1, r1, rows, chunks)
     gt.start()
     if halving:
@@ -696,7 +711,7 @@
             if n < len(pieces) // 2:
                 gu_o[:, k * width : (k + 1) * width] = hf[n].take_three()
             else:
-                gd_o[k * width : (k + 1) * width, :] = hf[n].take_three().T
+                gd_o[:, k * width : (k + 1) * width] = hf[n].take_three()
     rz = Scatter(ZP, ZOWN, ZPRE, ZYIN, s2, r2, rows, chunks)
     loads[2].wait()
     for k in range(chunks):
@@ -796,32 +811,6 @@
             hf[3].take_one()
     rd = Scatter(DATT, OWN, PRE, YIN, s3, r3, rows, chunks)
 
-    def head_grads(n, carry):
-        here = block(order_of(n, (far, yp, sib, t)), rows)
-        total = mm(DP[0, here, :], WQ[0], NT)
-        for c, ref in ((1, DK), (2, DV)):
-            part = jnp.concatenate([fold(ref[h, here, :]) for h in range(heads)], axis=1)
-            DP[c, here, :] = part
-            total = total + mm(part, WQ[c], NT)
-        DATT[here, :] = total
-
-        @pl.when(n == 0)
-        def _():
-            for k in range(chunks):
-                rd.send_pre(k)
-
-        @pl.when(n == 1)
-        def _():
-            for k in range(chunks):
-                rd.send_across(k)
-
-        @pl.when(n == 2)
-        def _():
-            rd.send_side()
-
-        return carry
-
-    lax.fori_loop(0, 4, head_grads, 0)
     rz.arrive()
 
     def out_rows(r):
@@ -833,6 +822,36 @@
     rz.finish_sends()
     a_copy = pltpu.make_async_copy(a_h, ZP, ls.at[8])
     a_copy.start()
+
+    def gather_heads(n, carry):
+        here = block(n, rows)
+        for c, ref in ((1, DK), (2, DV)):
+            DP[c, here, :] = jnp.concatenate([fold(ref[h, here, :]) for h in range(heads)], axis=1)
+        return carry
+
+    lax.fori_loop(0, 4, gather_heads, 0)
+
+    def head_grads(n, carry):
+        here = block(order_of(n, (far, yp, sib, t)), rows)
+        DATT[here, :] = mm(DP[0, here, :], WQ[0]) + mm(DP[1, here, :], WQ[1]) + mm(DP[2, here, :], WQ[2])
+
+        @pl.when(n == 0)
+        def _():
+            for k in range(chunks):
+                rd.send_pre(k)
+
+        @pl.when(n == 1)
+        def _():
+            for k in range(chunks):
+                rd.send_across(k)
+
+        @pl.when(n == 2)
+        def _():
+            rd.send_side()
+
+        return carry
+
+    lax.fori_loop(0, 2, head_grads, 0)
     a_copy.wait()
 
     def weight_grads(c, carry):
@@ -852,6 +871,7 @@
         return carry
 
     lax.fori_loop(0, 3, weight_grads, 0)
+    lax.fori_loop(2, 4, head_grads, 0)
     if halving:
         hf[3].take_two()
         ff_out(2)
@@ -896,9 +916,9 @@
         if halving and n == 0:
             hq[2].take_two()
         if halving and n == 1:
-            gq_o[:, 0, :] = hq[0].take_three()
+            gq_o[0] = hq[0].take_three()
         if halving and n == 2:
-            gq_o[:, 1, :] = hq[1].take_three()
+            gq_o[1] = hq[1].take_three()
         c.wait_recv()
         VB[n + 1] = VB[n] + VIN[n]
         rounds.append(c)
@@ -910,7 +930,7 @@
             def _():
                 vec_o[...] = VB[len(others), :, k * share : (k + 1) * share]
 
-        gq_o[:, 2, :] = hq[2].take_three()
+        gq_o[2] = hq[2].take_three()
         for h in hf + [ht] + hq:
             h.finish_sends()
     else:
@@ -935,11 +955,11 @@
     scratch = [
         cat, cat, cat, cat, vm(heads, 1, slots), vm(heads, 8, QB), vm(slots, feats), vm(heads, QB, 2 * HD), wide, wide, vm(3, slots, local),
         vm(rows, feats), vm(rows, feats), vm(rows, feats), vm(slots, feats), vm(rows, feats), vm(rows, feats), vm(rows, feats),
-        vm(3, feats, local), vm(local, feats), vm(16 + 8 * PASSES_MAX, feats), vm(ends + 1, 16, feats), vm(ends, 16, feats),
+        vm(3, local, feats), vm(local, feats), vm(16 + 8 * PASSES_MAX, feats), vm(ends + 1, 16, feats), vm(ends, 16, feats),
     ]
     sems = pairs(2, ng, ng, ng, ends) + pairs(1, 25)
     if halving:
-        outs += [struct(local, share), struct(share, 3, local), struct(hidden, share), struct(share, hidden)]
+        outs += [struct(local, share), struct(3, share, local), struct(share, hidden), struct(share, hidden)]
         args += [gd.reshape(8, share, hidden), gu.reshape(8, share, hidden)]
         scratch += [vm(8, share, local), vm(3, 8, share, local)]
         width = hidden // 2
@@ -969,8 +989,9 @@
     slots = rows * lax.axis_size("tensor")
     ways = lax.axis_size("dp")
     halving = ways == 8
-    a, qc, kc, vc, o, lse, wq, h1, c, dz = forward_call(
-        passes, x, pass_table, gain_one, bias_one, gain_two, bias_two, go, w_qkv, w_out, slots
+    wq = jnp.transpose(w_qkv, (1, 2, 0))
+    a, qc, kc, vc, o, lse, h1, c, dz = forward_call(
+        passes, x, pass_table, gain_one, bias_one, gain_two, bias_two, go, wq, w_out, slots
     )
     dh1, vec2, zp, gd, gu = middle_call(h1, go, gain_two, c, dz, w_up, w_down)
     got = backward_call(passes, x, pass_table, gain_one, h1, dh1, vec2, qc, kc, vc, o, lse, a, zp, wq, w_out, gd, gu, halving)
@@ -978,12 +999,11 @@
     if halving:
         gd, gu = got[5:]
     else:
-        gq = jnp.swapaxes(gq, 0, 1)
-        gt, gq, gu, gd = (lax.psum_scatter(v, "dp", scatter_dimension=0, tiled=True) for v in (gt, gq, gu, gd))
+        gt, gq, gu, gd = (lax.psum_scatter(v, "dp", scatter_dimension=0, tiled=True) for v in (gt, jnp.swapaxes(gq, 0, 1), gu, gd))
         part = lax.psum_scatter(part, "dp", scatter_dimension=1, tiled=True)
-        gt, gd = gt.T, gd.T
+        gt, gq = gt.T, jnp.swapaxes(gq, 0, 1)
     return (
-        out[None], gi[None], part[4 : 4 + PASSES_MAX], part[0], part[1], gq, gt, part[2], part[3], gu, gd,
+        out[None], gi[None], part[4 : 4 + PASSES_MAX], part[0], part[1], jnp.swapaxes(gq, 0, 1), gt, part[2], part[3], gu, gd.T,
     )
 
 

time: 267 us -> 254 us (0.951)
  local copies, waits for them, and re-layouts: 15.1 us -> 8.66 us
  Pallas kernels: 250 us -> 244 us
    unnamed x13 -> x16, local copies, waits for them, and re-layouts: 12.4 us -> 6.02 us
    pallas_call x1, Pallas kernels: 119 us -> 115 us  [backward_call(): pl.pallas_call(functools.partial(backward_kernel, (rows, slots, feats, he...]
where the time goes in v1:
time: 254 us
  Pallas kernels  244 us (96%)
  local copies, waits for them, and re-layouts  8.66 us (3%)
    pallas_call x1, Pallas kernels, backward_call(): pl.pallas_call(functools.partial(backward_kernel, (rows, slots, feats, he...  115 us
    pallas_call x1, Pallas kernels, forward_call(): pl.pallas_call(functools.partial(forward_kernel, (rows, slots, feats, hea...  73.7 us
    pallas_call x1, Pallas kernels, middle_call(): pl.pallas_call(functools.partial(middle_kernel, (rows, slots, feats, CHUN...  54.9 us
    unnamed x16, local copies, waits for them, and re-layouts  6.02 us

profile of v1, /device:TPU:0, one launch (start us, length us, event | category | flops | bytes accessed | tf_op | source)
XLA Modules:
  0.0 253.6 jit_solution(17685389315412668484)
XLA Ops:
  1.3 73.7 %forward_part.1 = (f32[1280,768]{1,0:T(8,128)}, bf16[3,1280,256]{2,1,0:T(8,128)(2,1)}, bf16[3,1280,256]{2,1,0:T(8,128)(2,1)}, bf16[3,1280,256]{2,1,0:T(8,128)(2,...) custom-call(s32[1]{0:T(128)S(6)} %copy.29.passes.refs_0_, ...), custom_call_target="tpu_custom_call" | custom-call | tf_op jit(solution)/shard_map/forward_part/pallas_call | solution.py:411
  75.0 54.9 %middle_part.1 = (f32[320,768]{1,0:T(8,128)}, f32[16,768]{1,0:T(8,128)}, f32[1280,768]{1,0:T(8,128)}, f32[768,768]{1,0:T(8,128)}, f32[768,768]{1,0:T(8,128)}) custom-call(f32[320,768]{1,0:T(8,128)} %get-tuple-element.32.h1.refs_4_, f32[320,768]{1,0:T(8,128)} %bitcast.22, f32[768]{0:T(1024)} %g2.3, f32[320,768]{1,0:T(8,128)} %get-tuple-element.33.c_h, ...), custom_call_target="tpu_custom_call" | custom-call | tf_op jit(solution)/shard_map/middle_part/pallas_call | solution.py:568
  130.0 114.9 %backward_part.1 = (f32[320,768]{1,0:T(8,128)}, f32[320,768]{1,0:T(8,128)}, f32[16,96]{1,0:T(8,128)}, f32[192,96]{1,0:T(8,128)}, f32[3,96,192]{2,1,0:T(8,128)}, /*index=5*/f32[96,768]{1,0:T(8,128)}, f32[96,768]{1,0:T(8,128)}) custom-call(s32[1]{0:T(128)S(6)} %copy.29.passes.refs_0_, f32[320,768]{1,0:T(8,128)} %bitcast.20, f32[5,768]{1,0:T(8,128)} %refs_2_.1, ...), custom_call_target="tpu_custom_call" | custom-call | tf_op jit(solution)/shard_map/backward_part/pallas_call | solution.py:973
  244.9 0.0 copy-start
  244.9 0.0 copy-start.3
  244.9 0.0 copy-start.4
  244.9 1.4 slice_bitcast_fusion
  246.3 1.3 slice.15
  247.6 0.0 copy-start.2
  247.6 0.0 copy-start.1
  247.6 2.3 copy.30
  249.8 0.0 copy-done
  249.8 0.9 copy.31
  250.8 0.0 copy-done.3
  250.8 0.7 copy.32
  251.5 0.0 copy-done.4
  251.5 0.6 copy.33
  252.1 0.0 copy-done.2
  252.1 0.7 copy.34
  252.9 0.0 copy-done.1
  252.9 0.7 copy.35
Async XLA Ops:
  244.9 4.9 %copy-start = (f32[320,768]{1,0:T(8,128)S(1)}, f32[320,768]{1,0:T(8,128)}, u32[]{:S(2)}) copy-start(f32[320,768]{1,0:T(8,128)} %get-tuple-element.47) | copy-start | bytes 2949124
  244.9 5.9 %copy-start.3 = (f32[3,96,192]{2,1,0:T(8,128)S(1)}, f32[3,96,192]{2,1,0:T(8,128)}, u32[]{:S(2)}) copy-start(f32[3,96,192]{2,1,0:T(8,128)} %get-tuple-element.49) | copy-start | bytes 663556
  244.9 6.6 %copy-start.4 = (f32[192,96]{1,0:T(8,128)S(1)}, f32[192,96]{1,0:T(8,128)}, u32[]{:S(2)}) copy-start(f32[192,96]{1,0:T(8,128)} %get-tuple-element.74) | copy-start | bytes 221188
  247.6 4.6 %copy-start.2 = (f32[96,768]{1,0:T(8,128)S(1)}, f32[96,768]{1,0:T(8,128)}, u32[]{:S(2)}) copy-start(f32[96,768]{1,0:T(8,128)} %get-tuple-element.77) | copy-start | bytes 884740
  247.6 5.3 %copy-start.1 = (f32[96,768]{1,0:T(8,128)S(1)}, f32[96,768]{1,0:T(8,128)}, u32[]{:S(2)}) copy-start(f32[96,768]{1,0:T(8,128)} %get-tuple-element.52) | copy-start | bytes 884740

commit v2 on v1

--- a/solution.py
+++ b/solution.py
@@ -428,6 +428,70 @@
     )(passes, x, table, g1, b1, g2, b2, go, wq, wo)
 
 
+FF_ORDERS = ((0, 1, 2), (1, 2, 0), (0, 1, 2), (0, 1, 2))
+Q_ORDERS = ((0, 1, 2), (1, 0, 2), (0, 1, 2))
+
+
+class Halve:
+    def __init__(self, source, keep, in_one, in_two, in_three, send, recv, base, order):
+        d = lax.axis_index("dp")
+        bits = (d % 2, (d // 2) % 2, d // 4)
+        peers = ({"dp": d + 1 - 2 * bits[0]}, {"dp": d + 2 - 4 * bits[1]}, {"dp": (d + 4) % 8})
+        a1, a2, a3 = order
+        self.mid, self.last = bits[a2], bits[a3]
+        self.spot = (lambda x, y: 2 * x + y) if a2 > a3 else (lambda x, y: 2 * y + x)
+        self.keep, self.ins = keep, (in_one, in_two, in_three)
+
+        def whole(v, x, y):
+            return v * 2**a1 + x * 2**a2 + y * 2**a3
+
+        pick = [(x, y) for x in range(2) for y in range(2)]
+        self.own = [(whole(bits[a1], x, y), self.spot(x, y)) for x, y in pick]
+        self.one = [
+            rcopy(source.at[whole(1 - bits[a1], x, y)], in_one.at[self.spot(x, y)], send.at[base + n], recv.at[base + n], peers[a1])
+            for n, (x, y) in enumerate(pick)
+        ]
+        if in_two is None:
+            return
+        self.two = [
+            rcopy(keep.at[self.spot(1 - self.mid, y)], in_two.at[y], send.at[base + 4 + y], recv.at[base + 4 + y], peers[a2])
+            for y in range(2)
+        ]
+        self.three = rcopy(keep.at[self.spot(self.mid, 1 - self.last)], in_three, send.at[base + 6], recv.at[base + 6], peers[a3])
+
+    def start_one(self):
+        for c in self.one:
+            c.start()
+
+    def add_one(self):
+        for c in self.one:
+            c.wait_recv()
+        self.keep[...] = self.keep[...] + self.ins[0][...]
+
+    def start_two(self):
+        for c in self.two:
+            c.start()
+
+    def take_one(self):
+        self.add_one()
+        self.start_two()
+
+    def take_two(self):
+        for y in range(2):
+            self.two[y].wait_recv()
+            at = self.spot(self.mid, y)
+            self.keep[at] = self.keep[at] + self.ins[1][y]
+        self.three.start()
+
+    def take_three(self):
+        self.three.wait_recv()
+        return self.keep[self.spot(self.mid, self.last)] + self.ins[2][...]
+
+    def finish_sends(self, first=True):
+        for c in (self.one if first else []) + self.two + [self.three]:
+            c.wait_send()
+
+
 def gelu_both(u):
     k = math.sqrt(2.0 / math.pi)
     square = u * u
@@ -437,13 +501,23 @@
     return u * half, slope
 
 
-def middle_kernel(
-    dims, h1, go, g2, c_h, dz_h, wu_h, wd_h,
-    dh1_o, vec_o, zp_o, gd_o, gu_o,
-    C, DZ, ACT, DU, PT, OWN, PRE, YIN, WU, WD, GD, GU,
-    s1, r1, s2, r2, ls,
-):
-    rows, slots, feats, chunks = dims
+def middle_kernel(dims, *refs):
+    rows, slots, feats, chunks, halving = dims
+    refs = list(refs)
+
+    def take(n):
+        out = refs[:n]
+        del refs[:n]
+        return out
+
+    h1, go, g2, c_h, dz_h, wu_h, wd_h = take(7)
+    dh1_o, vec_o, zp_o, gd_o, gu_o = take(5)
+    C, DZ, ACT, DU, PT, OWN, PRE, YIN, WU, WD, GD, GU = take(12)
+    if halving:
+        KG, G1 = take(2)
+    s1, r1, s2, r2, ls = take(5)
+    if halving:
+        sh, rh = take(2)
     t, sib, yp, far = places()
     first = pltpu.make_async_copy(c_h, C.at[block(t, rows)], ls.at[0])
     loads = [
@@ -455,6 +529,9 @@
     for c in loads:
         c.start()
     others = [{"tensor": sib}, {"tensor": yp}]
+    if halving:
+        d = lax.axis_index("dp")
+        others += [{"dp": d + 1 - 2 * (d % 2)}, {"dp": d + 2 - 4 * ((d // 2) % 2)}]
     greet(others)
     gc = Gather(C, s1, r1, rows, chunks, c_h)
     met(others)
@@ -519,15 +596,29 @@
 
     lax.fori_loop(0, 4 + 2 * chunks, step, 0)
 
-    def grads(n, carry):
-        cols = pl.ds(pl.multiple_of(n * 256, 256), 256)
-        GU[cols, :] = mm(C[:, cols], DU[...], TN)
-        GD[cols, :] = mm(DZ[:, cols], ACT[...], TN)
-        return carry
-
-    lax.fori_loop(0, feats // 256, grads, 0)
-    gu_copy = pltpu.make_async_copy(GU, gu_o, ls.at[4])
-    gu_copy.start()
+    def grads(left, right, out):
+        def step(n, carry):
+            cols = pl.ds(pl.multiple_of(n * (feats // 2), 128), feats // 2)
+            out[pl.ds(4 * n, 4)] = mm(left[:, cols], right[...], TN).reshape(4, feats // 8, feats)
+            return carry
+
+        lax.fori_loop(0, 2, step, 0)
+
+    grads(C, DU, GU)
+    if halving:
+        width = KG.shape[-1]
+        hg = []
+        for n in range(2):
+            half = GU.at[:, :, pl.ds(n * width, width)]
+            hg.append(Halve(half, KG.at[n], G1.at[n], None, None, sh, rh, 4 * n, FF_ORDERS[n]))
+            hg[n].start_one()
+        for n in range(2):
+            for a, b in hg[n].own:
+                KG[n, b] = GU[a, :, n * width : (n + 1) * width]
+    else:
+        gu_copy = pltpu.make_async_copy(GU, gu_o, ls.at[4])
+        gu_copy.start()
+    grads(DZ, ACT, GD)
     gd_copy = pltpu.make_async_copy(GD, gd_o, ls.at[5])
     gd_copy.start()
 
@@ -554,87 +645,43 @@
         dh1_o[here, :] = go[here, :] + inner * scale
 
     over_rows(rows, end_rows)
+    if halving:
+        for h in hg:
+            h.add_one()
+        gu_copy = pltpu.make_async_copy(KG, gu_o, ls.at[4])
+        gu_copy.start()
+        for h in hg:
+            for c in h.one:
+                c.wait_send()
     for c in (gu_copy, gd_copy, zp_copy):
         c.wait()
     gc.finish_sends()
     rs.finish_sends()
 
 
-def middle_call(h1, go, g2, c, dz, wu, wd):
+def middle_call(h1, go, g2, c, dz, wu, wd, halving):
     rows, feats = h1.shape
     slots = dz.shape[0]
     hidden = wu.shape[1]
     ng = 1 + 2 * CHUNKS
+    share = feats // 8
+    part = (2, 4, share, hidden // 2)
+    grad = (8, share, hidden)
     return pl.pallas_call(
-        functools.partial(middle_kernel, (rows, slots, feats, CHUNKS)),
-        out_shape=(struct(rows, feats), struct(16, feats), struct(slots, feats), struct(feats, hidden), struct(feats, hidden)),
+        functools.partial(middle_kernel, (rows, slots, feats, CHUNKS, halving)),
+        out_shape=(
+            struct(rows, feats), struct(16, feats), struct(slots, feats), struct(*grad), struct(*(part if halving else grad)),
+        ),
         in_specs=[IN_VMEM] * 3 + [IN_HBM] * 4,
         out_specs=(IN_VMEM, IN_VMEM, IN_HBM, IN_HBM, IN_HBM),
         scratch_shapes=[
             vm(slots, feats), vm(slots, feats), vm(slots, hidden), vm(slots, hidden), vm(slots, feats),
             vm(rows, feats), vm(rows, feats), vm(rows, feats),
-            vm(feats, hidden), vm(hidden, feats), vm(feats, hidden), vm(feats, hidden),
-        ] + pairs(2, ng, ng) + pairs(1, 7),
+            vm(feats, hidden), vm(hidden, feats), vm(*grad), vm(*grad),
+        ] + ([vm(*part), vm(*part)] if halving else []) + pairs(2, ng, ng) + pairs(1, 7) + (pairs(2, 8) if halving else []),
         compiler_params=params(2),
         name="middle_part",
     )(h1, go, g2, c, dz, wu, wd)
-
-
-FF_ORDERS = ((0, 1, 2), (1, 2, 0), (0, 1, 2), (0, 1, 2))
-FF_START = (1, 0, 2, 3)
-Q_ORDERS = ((0, 1, 2), (1, 0, 2), (0, 1, 2))
-
-
-class Halve:
-    def __init__(self, source, keep, in_one, in_two, in_three, send, recv, base, order):
-        d = lax.axis_index("dp")
-        bits = (d % 2, (d // 2) % 2, d // 4)
-        peers = ({"dp": d + 1 - 2 * bits[0]}, {"dp": d + 2 - 4 * bits[1]}, {"dp": (d + 4) % 8})
-        a1, a2, a3 = order
-        self.mid, self.last = bits[a2], bits[a3]
-        self.spot = (lambda x, y: 2 * x + y) if a2 > a3 else (lambda x, y: 2 * y + x)
-        self.keep, self.ins = keep, (in_one, in_two, in_three)
-
-        def whole(v, x, y):
-            return v * 2**a1 + x * 2**a2 + y * 2**a3
-
-        pick = [(x, y) for x in range(2) for y in range(2)]
-        self.own = [(whole(bits[a1], x, y), self.spot(x, y)) for x, y in pick]
-        self.one = [
-            rcopy(source.at[whole(1 - bits[a1], x, y)], in_one.at[self.spot(x, y)], send.at[base + n], recv.at[base + n], peers[a1])
-            for n, (x, y) in enumerate(pick)
-        ]
-        self.two = [
-            rcopy(keep.at[self.spot(1 - self.mid, y)], in_two.at[y], send.at[base + 4 + y], recv.at[base + 4 + y], peers[a2])
-            for y in range(2)
-        ]
-        self.three = rcopy(keep.at[self.spot(self.mid, 1 - self.last)], in_three, send.at[base + 6], recv.at[base + 6], peers[a3])
-
-    def start_one(self):
-        for c in self.one:
-            c.start()
-
-    def take_one(self):
-        for c in self.one:
-            c.wait_recv()
-        self.keep[...] = self.keep[...] + self.ins[0][...]
-        for c in self.two:
-            c.start()
-
-    def take_two(self):
-        for y in range(2):
-            self.two[y].wait_recv()
-            at = self.spot(self.mid, y)
-            self.keep[at] = self.keep[at] + self.ins[1][y]
-        self.three.start()
-
-    def take_three(self):
-        self.three.wait_recv()
-        return self.keep[self.spot(self.mid, self.last)] + self.ins[2][...]
-
-    def finish_sends(self):
-        for c in self.one + self.two + [self.three]:
-            c.wait_send()
 
 
 def backward_kernel(dims, *refs):
@@ -673,13 +720,15 @@
         d = lax.axis_index("dp")
         low = d % 2
         width = KF.shape[-1]
-        pieces = [(ref, k) for ref in (gu_h, gd_h) for k in range(ref.shape[-1] // width)]
         hf = []
-        for n, (ref, k) in enumerate(pieces):
-            ref = ref.at[:, :, pl.ds(k * width, width)]
-            hf.append(Halve(ref, KF.at[n], F1.at[n], F2.at[n], F3.at[n], sh, rh, 7 * n, FF_ORDERS[n]))
+        for n in range(4):
+            ref = gd_h.at[:, :, pl.ds(n % 2 * width, width)]
+            hf.append(Halve(ref, KF.at[n], F1.at[n // 2 * (n - 2)], F2.at[n], F3.at[n], sh, rh, 7 * n, FF_ORDERS[n]))
+        loads += [pltpu.make_async_copy(gu_h.at[n], KF.at[n], ls.at[9 + n]) for n in range(2)]
+        for n in (2, 3):
+            ref = gd_h.at[:, :, pl.ds(n % 2 * width, width)]
             loads += [
-                pltpu.make_async_copy(ref.at[a], KF.at[n, b], ls.at[9 + 4 * n + m]) for m, (a, b) in enumerate(hf[n].own)
+                pltpu.make_async_copy(ref.at[a], KF.at[n, b], ls.at[3 + 4 * n + m]) for m, (a, b) in enumerate(hf[n].own)
             ]
         early = loads[8:]
     for c in loads:
@@ -700,15 +749,19 @@
     gt = Gather(DATT, s1, r1, rows, chunks)
     gt.start()
     if halving:
-        for n in FF_START:
+        for n in (2, 3):
             hf[n].start_one()
-        base = 7 * len(pieces)
+        for c in early[:2]:
+            c.wait()
+        hf[0].start_two()
+        hf[1].start_two()
+        base = 28
         ht = Halve(GT, KT, T1, T2, T3, sh, rh, base, (0, 1, 2))
         hq = [Halve(GQ.at[c], KQ.at[c], Q1.at[c], Q2.at[c], Q3.at[c], sh, rh, base + 7 + 7 * c, Q_ORDERS[c]) for c in range(3)]
 
         def ff_out(n):
-            k = n % (len(pieces) // 2)
-            if n < len(pieces) // 2:
+            k = n % 2
+            if n < 2:
                 gu_o[:, k * width : (k + 1) * width] = hf[n].take_three()
             else:
                 gd_o[:, k * width : (k + 1) * width] = hf[n].take_three()
@@ -731,10 +784,11 @@
             for k in range(chunks):
                 rz.send_across(k)
             if halving:
-                for c in early:
+                for c in early[2:]:
                     c.wait()
-                hf[0].take_one()
-                hf[1].take_one()
+                hf[0].take_two()
+                hf[1].take_two()
+                hf[2].take_one()
 
         @pl.when(n == 3)
         def _():
@@ -798,17 +852,18 @@
         dq = jnp.concatenate([fold(DQ[h]) for h in range(heads)], axis=1)
         DP[0, q_rows, :] = dq * (1.0 / math.sqrt(HD))
         if halving and i == 4:
-            hf[0].take_two()
-            hf[1].take_two()
+            ff_out(0)
+            hf[3].take_one()
         if halving and i == 3:
-            hf[2].take_one()
+            hf[2].take_two()
+            ff_out(1)
         if halving and i == 2:
-            ff_out(0)
+            ht.take_one()
         if halving and i == 1:
-            ff_out(1)
-            hf[2].take_two()
+            hf[3].take_two()
+            ff_out(2)
         if halving and i == 0:
-            hf[3].take_one()
+            ht.take_two()
     rd = Scatter(DATT, OWN, PRE, YIN, s3, r3, rows, chunks)
 
     rz.arrive()
@@ -873,17 +928,12 @@
     lax.fori_loop(0, 3, weight_grads, 0)
     lax.fori_loop(2, 4, head_grads, 0)
     if halving:
-        hf[3].take_two()
-        ff_out(2)
-        ht.take_one()
+        ff_out(3)
         hq[1].take_one()
         hq[0].take_one()
-        ff_out(3)
-        ht.take_two()
         hq[1].take_two()
         hq[0].take_two()
         hq[2].take_one()
-        gt_o[...] = ht.take_three().T
     ACC[...] = jnp.zeros_like(ACC)
     gain1 = row_of(g1)
     rd.arrive()
@@ -915,6 +965,7 @@
         c.start()
         if halving and n == 0:
             hq[2].take_two()
+            gt_o[...] = ht.take_three().T
         if halving and n == 1:
             gq_o[0] = hq[0].take_three()
         if halving and n == 2:
@@ -931,8 +982,8 @@
                 vec_o[...] = VB[len(others), :, k * share : (k + 1) * share]
 
         gq_o[2] = hq[2].take_three()
-        for h in hf + [ht] + hq:
-            h.finish_sends()
+        for n, h in enumerate(hf + [ht] + hq):
+            h.finish_sends(n >= 2)
     else:
         vec_o[...] = VB[len(others)]
     for c in rounds:
@@ -944,7 +995,7 @@
     rows, feats = x.shape
     slots, local = o.shape
     heads = local // HD
-    hidden = gd.shape[1]
+    hidden = gd.shape[2]
     ng = 1 + 2 * CHUNKS
     ends = 5 if halving else 2
     share = feats // 8
@@ -960,11 +1011,11 @@
     sems = pairs(2, ng, ng, ng, ends) + pairs(1, 25)
     if halving:
         outs += [struct(local, share), struct(3, share, local), struct(share, hidden), struct(share, hidden)]
-        args += [gd.reshape(8, share, hidden), gu.reshape(8, share, hidden)]
+        args += [gd, gu]
         scratch += [vm(8, share, local), vm(3, 8, share, local)]
         width = hidden // 2
         scratch += [vm(4, 4, share, width), vm(4, share, local), vm(3, 4, share, local)]
-        scratch += [vm(4, 4, share, width), vm(4, 2, share, width), vm(4, share, width)]
+        scratch += [vm(2, 4, share, width), vm(4, 2, share, width), vm(4, share, width)]
         scratch += [vm(4, share, local), vm(2, share, local), vm(share, local)]
         scratch += [vm(3, 4, share, local), vm(3, 2, share, local), vm(3, share, local)]
         sems += pairs(2, 56)
@@ -981,6 +1032,40 @@
     )(*args)
 
 
+def finish_kernel(*refs):
+    srcs, part_h, dsts, small = refs[:6], refs[6], refs[7:13], refs[13:18]
+    bufs, part, sem_in, sem_out = refs[18:24], refs[24], refs[25], refs[26]
+    into = [pltpu.make_async_copy(a, b, sem_in.at[n]) for n, (a, b) in enumerate(zip(srcs, bufs))]
+    into.append(pltpu.make_async_copy(part_h, part, sem_in.at[6]))
+    out = [pltpu.make_async_copy(b, a, sem_out.at[n]) for n, (b, a) in enumerate(zip(bufs, dsts))]
+    for c in into:
+        c.start()
+    for a, b in zip(into, out):
+        a.wait()
+        b.start()
+    into[6].wait()
+    small[0][...] = part[4 : 4 + PASSES_MAX, :]
+    for n in range(4):
+        small[1 + n][...] = part[n, :]
+    for c in out:
+        c.wait()
+
+
+def finish_call(out, gi, part, gt, gq, gd, gu):
+    share = part.shape[1]
+    big = (out, gi, gt, gq, gd, gu)
+    got = pl.pallas_call(
+        finish_kernel,
+        out_shape=tuple(struct(*v.shape) for v in big) + (struct(PASSES_MAX, share),) + (struct(share),) * 4,
+        in_specs=[IN_HBM] * 7,
+        out_specs=(IN_HBM,) * 6 + (IN_VMEM,) * 5,
+        scratch_shapes=[vm(*v.shape) for v in big] + [vm(*part.shape)] + pairs(1, 7, 6),
+        compiler_params=pltpu.CompilerParams(vmem_limit_bytes=63 << 20),
+        name="finish_part",
+    )(*big, part)
+    return got[:2] + got[6:] + got[2:6]
+
+
 def per_device(
     block_input, passes, pass_map, pass_table, gain_one, bias_one, w_qkv, w_out, gain_two, bias_two, w_up, w_down, grad_output
 ):
@@ -993,17 +1078,19 @@
     a, qc, kc, vc, o, lse, h1, c, dz = forward_call(
         passes, x, pass_table, gain_one, bias_one, gain_two, bias_two, go, wq, w_out, slots
     )
-    dh1, vec2, zp, gd, gu = middle_call(h1, go, gain_two, c, dz, w_up, w_down)
+    dh1, vec2, zp, gd, gu = middle_call(h1, go, gain_two, c, dz, w_up, w_down, halving)
     got = backward_call(passes, x, pass_table, gain_one, h1, dh1, vec2, qc, kc, vc, o, lse, a, zp, wq, w_out, gd, gu, halving)
     out, gi, part, gt, gq = got[:5]
     if halving:
-        gd, gu = got[5:]
+        out, gi, table, ga, ba, gb, bb, gt, gq, gd, gu = finish_call(out, gi, part, gt, gq, *got[5:])
     else:
+        gd, gu = gd.reshape(feats, -1), gu.reshape(feats, -1)
         gt, gq, gu, gd = (lax.psum_scatter(v, "dp", scatter_dimension=0, tiled=True) for v in (gt, jnp.swapaxes(gq, 0, 1), gu, gd))
         part = lax.psum_scatter(part, "dp", scatter_dimension=1, tiled=True)
         gt, gq = gt.T, jnp.swapaxes(gq, 0, 1)
+        table, ga, ba, gb, bb = part[4 : 4 + PASSES_MAX], part[0], part[1], part[2], part[3]
     return (
-        out[None], gi[None], part[4 : 4 + PASSES_MAX], part[0], part[1], jnp.swapaxes(gq, 0, 1), gt, part[2], part[3], gu, gd.T,
+        out[None], gi[None], table, ga, ba, jnp.swapaxes(gq, 0, 1), gt, gb, bb, gu, gd.T,
     )
 
 

time: 254 us -> 249 us (0.980)
  local copies, waits for them, and re-layouts: 8.66 us -> 0 us
  Pallas kernels: 244 us -> 247 us
    unnamed x16 -> x0, local copies, waits for them, and re-layouts: 6.02 us -> none
    pallas_call x0 -> x1, Pallas kernels: none -> 3.51 us  [finish_call(): pl.pallas_call(finish_kernel, out_shape=tuple((struct(*v.shape) for v in...]
where the time goes in v2:
time: 249 us; the launch traced here: 248 us
  Pallas kernels  247 us (99%)
    pallas_call x1, Pallas kernels, backward_call(): pl.pallas_call(functools.partial(backward_kernel, (rows, slots, feats, he...  113 us
    pallas_call x1, Pallas kernels, forward_call(): pl.pallas_call(functools.partial(forward_kernel, (rows, slots, feats, hea...  73.8 us
    pallas_call x1, Pallas kernels, middle_call(): pl.pallas_call(functools.partial(middle_kernel, (rows, slots, feats, CHUN...  56.2 us

profile of v2, /device:TPU:0, one launch (start us, length us, event | category | flops | bytes accessed | tf_op | source)
XLA Modules:
  0.0 248.3 jit_solution(598252814777609433)
XLA Ops:
  1.3 73.8 %forward_part.1 = (f32[1280,768]{1,0:T(8,128)}, bf16[3,1280,256]{2,1,0:T(8,128)(2,1)}, bf16[3,1280,256]{2,1,0:T(8,128)(2,1)}, bf16[3,1280,256]{2,1,0:T(8,128)(2,...) custom-call(s32[1]{0:T(128)S(6)} %copy.23.passes.refs_0_, ...), custom_call_target="tpu_custom_call" | custom-call | tf_op jit(solution)/shard_map/forward_part/pallas_call | solution.py:411
  75.1 56.2 %middle_part.1 = (f32[320,768]{1,0:T(8,128)}, f32[16,768]{1,0:T(8,128)}, f32[1280,768]{1,0:T(8,128)}, f32[8,96,768]{2,1,0:T(8,128)}, f32[2,4,96,384]{3,2,1,0:T(8,128)}) custom-call(f32[320,768]{1,0:T(8,128)} %get-tuple-element.43.refs_0_.refs_4_, f32[320,768]{1,0:T(8,128)} %bitcast.12, f32[768]{0:T(1024)} %refs_2_.2, f32[320,768]{1,0:T(8,128)} %get-tuple-element.44.refs_3_, ...), custom_call_target="tpu_custom_call" | custom-call | tf_op jit(solution)/shard_map/middle_part/pallas_call | solution.py:670
  131.3 113.3 %backward_part.1 = (f32[320,768]{1,0:T(8,128)}, f32[320,768]{1,0:T(8,128)}, f32[16,96]{1,0:T(8,128)}, f32[192,96]{1,0:T(8,128)}, f32[3,96,192]{2,1,0:T(8,128)}, /*index=5*/f32[96,768]{1,0:T(8,128)}, f32[96,768]{1,0:T(8,128)}) custom-call(s32[1]{0:T(128)S(6)} %copy.23.passes.refs_0_, f32[320,768]{1,0:T(8,128)} %bitcast.10, f32[5,768]{1,0:T(8,128)} %refs_2_.3, ...), custom_call_target="tpu_custom_call" | custom-call | tf_op jit(solution)/shard_map/backward_part/pallas_call | solution.py:1024
  244.6 3.5 %finish_part.1 = (f32[320,768]{1,0:T(8,128)}, f32[320,768]{1,0:T(8,128)}, f32[192,96]{1,0:T(8,128)}, f32[3,96,192]{2,1,0:T(8,128)}, f32[96,768]{1,0:T(8,128)}, /...) custom-call(f32[320,768]{1,0:T(8,128)} %get-tuple-element.57.refs_0_, ...), custom_call_target="tpu_custom_call" | custom-call | tf_op jit(solution)/shard_map/finish_part/pallas_call | solution.py:1057
